TPU v7x, 32 devices: a whole 2x2x4 slice. The times are simulated.
32 devices in a mesh: cand: 4 (over x, core), tp: 8 (over z, y).
Axes of the slice: x: 2, y: 2, z: 4, core: 2. Of those that a mesh axis runs over, the one named last changes fastest.
Arguments:
- start_state: float32 [128], replicated, may hold values from -6 to 6
- goal: float32 [128], replicated, may hold values from -6 to 6
- mean_prev: float32 [128], replicated, may hold values from -0.5 to 0.5
- std_prev: float32 [128], replicated, may hold values from 0.1 to 0.5
- noise: float32 [768, 128], P('cand'), may hold values from -23 to 23
- members: int32 [768, 1], P('cand'), may hold values from 0 to 3; in each aligned block of 192 rows (0 to 191, 192 to 383, ...) at most 60 rows name the same one
- elites: int32 [96], replicated, may hold values from 0 to 767, as said below
- w_in: bfloat16 [4, 144, 4096], P(None, None, 'tp'), may hold values from -0.5 to 0.5
- w_hid: bfloat16 [4, 4096, 4096], P(None, None, 'tp'), may hold values from -0.09375 to 0.09375
- w_out: bfloat16 [4, 4096, 128], P(None, 'tp'), may hold values from -0.09375 to 0.09375
Outputs:
- scores: float32 [768], P('cand')
- new_mean: float32 [128], replicated
- new_std: float32 [128], replicated
Inputs may be any that keep to these rules, and one draw needn't show every extreme that they name: `members`: among the candidates of one index of cand no member is named more than 60 times. `elites`: 96 distinct candidate numbers.
All inputs are finite; a program needn't handle non-finite values.
Results may differ from a plain program's by a relative error of at most 0.0085.
Values may be sent and summed in bfloat16 or wider, within the bound.
A program may use at most 64 MiB of HBM per device.

v0:
```python
import jax
import jax.numpy as jnp
from jax import lax
from jax.sharding import PartitionSpec as P

HORIZON = 8


def reward_of(states, goal, action):
    return -jnp.mean((states - goal) ** 2, axis=-1) - 0.1 * jnp.mean(action * action, axis=-1)


def on_device(start_state, goal, mean_prev, std_prev, noise, members, elites, w_in, w_hid, w_out):
    local_count = noise.shape[0]
    member_count = w_in.shape[0]
    state_width = start_state.shape[0]
    capacity = 5 * local_count // 16
    action_width = mean_prev.shape[0] // HORIZON
    actions = mean_prev[None, :] + std_prev[None, :] * noise
    onehot = (members == jnp.arange(member_count, dtype=jnp.int32)[None, :]).astype(jnp.float32)
    before = jnp.cumsum(onehot, axis=0) - onehot
    position = jnp.sum(before * onehot, axis=1).astype(jnp.int32)
    slot_number = members[:, 0] * capacity + position
    dispatch = (
        slot_number[None, :] == jnp.arange(member_count * capacity, dtype=jnp.int32)[:, None]
    ).astype(jnp.float32)
    slot_actions = jnp.dot(dispatch, actions, precision=lax.Precision.HIGHEST)
    slot_actions = slot_actions.reshape(member_count, capacity, HORIZON, action_width)
    input_layer = lax.all_gather(w_in, "tp", axis=2, tiled=True)

    def rollout(first, count):
        layer_in = input_layer[first : first + count]
        hid_rows = w_hid[first : first + count]
        out_rows = w_out[first : first + count]
        states = jnp.zeros((count, capacity, state_width), jnp.float32) + start_state[None, None, :]
        running = jnp.zeros((count, capacity), jnp.float32)
        for step_index in range(HORIZON):
            action = slot_actions[first : first + count, :, step_index, :]
            inputs = jnp.concatenate([states, action], axis=2).astype(jnp.bfloat16)
            first_pre = jnp.einsum(
                "mck,mkh->mch", inputs, layer_in, preferred_element_type=jnp.float32
            )
            hidden_one = jax.nn.silu(first_pre).astype(jnp.bfloat16)
            second_pre = jnp.einsum(
                "mck,mkh->mch", hidden_one, hid_rows, preferred_element_type=jnp.float32
            )
            hidden_two = jax.nn.silu(second_pre).astype(jnp.bfloat16)
            partial_change = jnp.einsum(
                "mck,mks->mcs", hidden_two, out_rows, preferred_element_type=jnp.float32
            )
            change = lax.psum(partial_change, "tp")
            states = states + change
            running = running + reward_of(states, goal[None, None, :], action)
        return running

    slot_returns = jnp.concatenate([rollout(member, 1) for member in range(member_count)], axis=0)
    returns = jnp.dot(
        slot_returns.reshape(member_count * capacity), dispatch, precision=lax.Precision.HIGHEST
    )
    first_index = lax.axis_index("cand") * local_count
    numbers = first_index + jnp.arange(local_count, dtype=jnp.int32)
    chosen = jnp.sum((elites[:, None] == numbers[None, :]).astype(jnp.float32), axis=0)
    count_all = local_count * lax.axis_size("cand")
    return_sum = lax.psum(jnp.sum(returns), "cand")
    return_mean = return_sum / count_all
    return_spread = lax.psum(jnp.sum((returns - return_mean) ** 2), "cand")
    return_var = return_spread / count_all
    scores = (returns - return_mean) / jnp.sqrt(return_var + 1e-06)
    weights = chosen * (0.5 + jax.nn.sigmoid(scores))
    weight_sum, first_moment = lax.psum(
        (jnp.sum(weights), jnp.dot(weights, actions, precision=lax.Precision.HIGHEST)), "cand"
    )
    new_mean = first_moment / weight_sum
    action_spread = lax.psum(
        jnp.dot(weights, (actions - new_mean[None, :]) ** 2, precision=lax.Precision.HIGHEST),
        "cand",
    )
    new_var = action_spread / weight_sum
    new_std = jnp.sqrt(new_var + 1e-06)
    return (scores, new_mean, new_std)


def solution(mesh):
    placed = (
        P(),
        P(),
        P(),
        P(),
        P("cand", None),
        P("cand", None),
        P(),
        P(None, None, "tp"),
        P(None, None, "tp"),
        P(None, "tp", None),
    )
    return jax.shard_map(
        on_device, mesh=mesh, in_specs=placed, out_specs=(P("cand"), P(), P()), check_vma=False
    )
```

profile of v0, /device:TPU:0, one launch (start us, length us, event | category | flops | bytes accessed | tf_op | source)
XLA Modules:
  0.0 847.4 jit_solution(5525363201203804489)
XLA Ops:
  8.7 1.2 reduce-window.6
  11.7 1.2 fusion.129
  16.0 77.4 %all-gather.2.cloned.1.call-done = bf16[4,144,4096]{2,1,0:T(8,128)(2,1)} async-done(((bf16[4,144,512]{2,1,0:T(8,128)(2,1)}), bf16[4,144,4096]{2,1,0:T(8,128)(2,1)}) %all-gather.2.cloned.1.call-update) | async-done | bytes 4718608 | tf_op jit(solution)/shard_map/all_gather | solution.py:29
  93.4 3.7 multiply_convert_fusion.109
  97.1 0.8 convolution_bitcast_fusion.15
  97.9 3.7 multiply_convert_fusion.133
  102.3 3.7 multiply_convert_fusion.157
  106.0 0.8 convolution_bitcast_fusion.31
  106.8 3.7 multiply_convert_fusion.85
  111.8 69.2 %all-reduce.33.cloned.1.call-done = (f32[1,60,128]{2,1,0:T(8,128)}, f32[1,60,128]{2,1,0:T(8,128)}, f32[1,60,128]{2,1,0:T(8,128)}, f32[1,60,128]{2,1,0:T(8,128)}) async-done(((f32[1,60,128]{2,1,0:T(8,128)}, f32[1,60,128]{2,1,0:T(8,128)}, f32[1,60,128]{2,1,0:T(8,128)}, f32[1,60,128]{2,1,0:T(8,128)}), (f32[1,60,128]{2,1,0:T(8,128)}, f32[1,60,128]{2,1,0:T(8,128)}, f32[1,60,128]{2,1,0:T(8,128)}, ...) | async-done | bytes 122896 | tf_op jit(solution)/shard_map/psum | solution.py:51
  180.9 0.8 fusion.485
  181.7 3.7 multiply_convert_fusion.154
  186.2 3.7 multiply_convert_fusion.82
  190.7 3.7 multiply_convert_fusion.106
  195.1 3.7 multiply_convert_fusion.130
  200.4 69.7 %all-reduce.31.cloned.1.call-done = (f32[1,60,128]{2,1,0:T(8,128)}, f32[1,60,128]{2,1,0:T(8,128)}, f32[1,60,128]{2,1,0:T(8,128)}, f32[1,60,128]{2,1,0:T(8,128)}) async-done(((f32[1,60,128]{2,1,0:T(8,128)}, f32[1,60,128]{2,1,0:T(8,128)}, f32[1,60,128]{2,1,0:T(8,128)}, f32[1,60,128]{2,1,0:T(8,128)}), (f32[1,60,128]{2,1,0:T(8,128)}, f32[1,60,128]{2,1,0:T(8,128)}, f32[1,60,128]{2,1,0:T(8,128)}, ...) | async-done | bytes 122896 | tf_op jit(solution)/shard_map/psum | solution.py:51
  270.1 0.8 convert_bitcast_fusion.50
  271.0 3.7 multiply_convert_fusion.151
  274.7 0.8 convolution_bitcast_fusion.29
  275.5 3.7 multiply_convert_fusion.79
  279.9 3.7 multiply_convert_fusion.103
  283.6 0.8 convolution_bitcast_fusion.13
  284.4 3.7 multiply_convert_fusion.127
  289.5 69.9 %all-reduce.29.cloned.1.call-done = (f32[1,60,128]{2,1,0:T(8,128)}, f32[1,60,128]{2,1,0:T(8,128)}, f32[1,60,128]{2,1,0:T(8,128)}, f32[1,60,128]{2,1,0:T(8,128)}) async-done(((f32[1,60,128]{2,1,0:T(8,128)}, f32[1,60,128]{2,1,0:T(8,128)}, f32[1,60,128]{2,1,0:T(8,128)}, f32[1,60,128]{2,1,0:T(8,128)}), (f32[1,60,128]{2,1,0:T(8,128)}, f32[1,60,128]{2,1,0:T(8,128)}, f32[1,60,128]{2,1,0:T(8,128)}, ...) | async-done | bytes 122896 | tf_op jit(solution)/shard_map/psum | solution.py:51
  359.4 0.8 convert_bitcast_fusion.35
  360.2 3.7 multiply_convert_fusion.148
  364.7 3.7 multiply_convert_fusion.76
  368.4 0.8 convolution_bitcast_fusion.4
  369.2 3.7 multiply_convert_fusion.100
  373.6 3.7 multiply_convert_fusion.124
  377.3 0.8 convolution_bitcast_fusion.20
  378.8 69.9 %all-reduce.27.cloned.1.call-done = (f32[1,60,128]{2,1,0:T(8,128)}, f32[1,60,128]{2,1,0:T(8,128)}, f32[1,60,128]{2,1,0:T(8,128)}, f32[1,60,128]{2,1,0:T(8,128)}) async-done(((f32[1,60,128]{2,1,0:T(8,128)}, f32[1,60,128]{2,1,0:T(8,128)}, f32[1,60,128]{2,1,0:T(8,128)}, f32[1,60,128]{2,1,0:T(8,128)}), (f32[1,60,128]{2,1,0:T(8,128)}, f32[1,60,128]{2,1,0:T(8,128)}, f32[1,60,128]{2,1,0:T(8,128)}, ...) | async-done | bytes 122896 | tf_op jit(solution)/shard_map/psum | solution.py:51
  449.4 3.7 multiply_convert_fusion.145
  453.9 3.7 multiply_convert_fusion.73
  457.6 0.8 convolution_bitcast_fusion.3
  458.4 3.7 multiply_convert_fusion.97
  462.1 0.8 convolution_bitcast_fusion.11
  462.9 3.7 multiply_convert_fusion.121
  466.6 0.8 convolution_bitcast_fusion.19
  468.3 69.7 %all-reduce.25.cloned.1.call-done = (f32[1,60,128]{2,1,0:T(8,128)}, f32[1,60,128]{2,1,0:T(8,128)}, f32[1,60,128]{2,1,0:T(8,128)}, f32[1,60,128]{2,1,0:T(8,128)}) async-done(((f32[1,60,128]{2,1,0:T(8,128)}, f32[1,60,128]{2,1,0:T(8,128)}, f32[1,60,128]{2,1,0:T(8,128)}, f32[1,60,128]{2,1,0:T(8,128)}), (f32[1,60,128]{2,1,0:T(8,128)}, f32[1,60,128]{2,1,0:T(8,128)}, f32[1,60,128]{2,1,0:T(8,128)}, ...) | async-done | bytes 122896 | tf_op jit(solution)/shard_map/psum | solution.py:51
  538.7 3.7 multiply_convert_fusion.142
  543.2 3.7 multiply_convert_fusion.70
  547.7 3.7 multiply_convert_fusion.94
  552.2 3.7 multiply_convert_fusion.118
  557.2 70.0 %all-reduce.23.cloned.1.call-done = (f32[1,60,128]{2,1,0:T(8,128)}, f32[1,60,128]{2,1,0:T(8,128)}, f32[1,60,128]{2,1,0:T(8,128)}, f32[1,60,128]{2,1,0:T(8,128)}) async-done(((f32[1,60,128]{2,1,0:T(8,128)}, f32[1,60,128]{2,1,0:T(8,128)}, f32[1,60,128]{2,1,0:T(8,128)}, f32[1,60,128]{2,1,0:T(8,128)}), (f32[1,60,128]{2,1,0:T(8,128)}, f32[1,60,128]{2,1,0:T(8,128)}, f32[1,60,128]{2,1,0:T(8,128)}, ...) | async-done | bytes 122896 | tf_op jit(solution)/shard_map/psum | solution.py:51
  628.0 3.7 multiply_convert_fusion.139
  632.5 3.7 multiply_convert_fusion.67
  637.0 3.7 multiply_convert_fusion.91
  641.4 3.7 multiply_convert_fusion.115
  646.1 70.3 %all-reduce.21.cloned.1.call-done = (f32[1,60,128]{2,1,0:T(8,128)}, f32[1,60,128]{2,1,0:T(8,128)}, f32[1,60,128]{2,1,0:T(8,128)}, f32[1,60,128]{2,1,0:T(8,128)}) async-done(((f32[1,60,128]{2,1,0:T(8,128)}, f32[1,60,128]{2,1,0:T(8,128)}, f32[1,60,128]{2,1,0:T(8,128)}, f32[1,60,128]{2,1,0:T(8,128)}), (f32[1,60,128]{2,1,0:T(8,128)}, f32[1,60,128]{2,1,0:T(8,128)}, f32[1,60,128]{2,1,0:T(8,128)}, ...) | async-done | bytes 122896 | tf_op jit(solution)/shard_map/psum | solution.py:51
  717.2 3.7 multiply_convert_fusion.136
  721.7 3.7 multiply_convert_fusion.64
  726.2 3.7 multiply_convert_fusion.88
  729.9 0.8 convolution_bitcast_fusion.8
  730.7 3.7 multiply_convert_fusion.112
  735.2 70.5 %all-reduce.19.cloned.1.call-done = (f32[1,60,128]{2,1,0:T(8,128)}, f32[1,60,128]{2,1,0:T(8,128)}, f32[1,60,128]{2,1,0:T(8,128)}, f32[1,60,128]{2,1,0:T(8,128)}) async-done(((f32[1,60,128]{2,1,0:T(8,128)}, f32[1,60,128]{2,1,0:T(8,128)}, f32[1,60,128]{2,1,0:T(8,128)}, f32[1,60,128]{2,1,0:T(8,128)}), (f32[1,60,128]{2,1,0:T(8,128)}, f32[1,60,128]{2,1,0:T(8,128)}, f32[1,60,128]{2,1,0:T(8,128)}, ...) | async-done | bytes 122896 | tf_op jit(solution)/shard_map/psum | solution.py:51
  805.8 1.2 multiply_reduce_fusion.59
  807.0 1.2 multiply_reduce_fusion.33
  809.2 6.3 psum.291
  816.8 7.2 psum.292
  824.8 1.2 fusion.595
  826.1 6.6 all-reduce.9
  833.6 6.0 psum.295
  839.7 1.2 add_sqrt_fusion
  (193 shorter events, 33.2 us)
Async XLA Ops:
  7.2 86.2 %all-gather.2.cloned.1.call-start = ((), (), s32[]{:S(2)}) async-start(), calls=%async_computation | async-start | bytes 5308416 | tf_op jit(solution)/shard_map/all_gather | solution.py:29
  7.9 173.0 %all-reduce.33.cloned.1.call-start = ((), (), s32[]{:S(2)}) async-start(), calls=%async_computation.8 | async-start | bytes 262144 | tf_op jit(solution)/shard_map/psum | solution.py:51
  93.4 3.7 copy-start
  106.8 74.1 %copy-start.22 = (f32[128]{0:T(128)S(1)}, f32[128]{0:T(128)}, u32[]{:S(2)}) copy-start(f32[128]{0:T(128)} %param.10) | copy-start | bytes 1540
  111.3 158.8 %all-reduce.31.cloned.1.call-start = ((), (), s32[]{:S(2)}) async-start(), calls=%async_computation.7 | async-start | bytes 262144 | tf_op jit(solution)/shard_map/psum | solution.py:51
  195.1 75.0 %copy-start.2 = (f32[1,60,128]{2,1,0:T(8,128)S(1)}, f32[1,60,128]{2,1,0:T(8,128)}, u32[]{:S(2)}) copy-start(f32[1,60,128]{2,1,0:T(8,128)} %get-tuple-element.73) | copy-start | bytes 92164
  195.1 75.0 %copy-start.3 = (f32[1,60,128]{2,1,0:T(8,128)S(1)}, f32[1,60,128]{2,1,0:T(8,128)}, u32[]{:S(2)}) copy-start(f32[1,60,128]{2,1,0:T(8,128)} %get-tuple-element.74) | copy-start | bytes 92164
  195.1 75.0 %copy-start.4 = (f32[1,60,128]{2,1,0:T(8,128)S(1)}, f32[1,60,128]{2,1,0:T(8,128)}, u32[]{:S(2)}) copy-start(f32[1,60,128]{2,1,0:T(8,128)} %get-tuple-element.75) | copy-start | bytes 92164
  195.1 75.0 %copy-start.5 = (f32[1,60,128]{2,1,0:T(8,128)S(1)}, f32[1,60,128]{2,1,0:T(8,128)}, u32[]{:S(2)}) copy-start(f32[1,60,128]{2,1,0:T(8,128)} %get-tuple-element.76) | copy-start | bytes 92164
  199.6 159.8 %all-reduce.29.cloned.1.call-start = ((), (), s32[]{:S(2)}) async-start(), calls=%async_computation.6 | async-start | bytes 262144 | tf_op jit(solution)/shard_map/psum | solution.py:51
  288.9 159.8 %all-reduce.27.cloned.1.call-start = ((), (), s32[]{:S(2)}) async-start(), calls=%async_computation.5 | async-start | bytes 262144 | tf_op jit(solution)/shard_map/psum | solution.py:51
  360.2 4.5 copy-start.12
  360.2 4.5 copy-start.13
  378.1 159.8 %all-reduce.25.cloned.1.call-start = ((), (), s32[]{:S(2)}) async-start(), calls=%async_computation.4 | async-start | bytes 262144 | tf_op jit(solution)/shard_map/psum | solution.py:51
  449.4 4.5 copy-start.17
  453.9 4.5 copy-start.11
  458.4 4.5 copy-start.8
  467.4 159.8 %all-reduce.23.cloned.1.call-start = ((), (), s32[]{:S(2)}) async-start(), calls=%async_computation.3 | async-start | bytes 262144 | tf_op jit(solution)/shard_map/psum | solution.py:51
  538.7 4.5 copy-start.15
  543.2 4.5 copy-start.9
  547.7 4.5 copy-start.6
  556.7 159.7 %all-reduce.21.cloned.1.call-start = ((), (), s32[]{:S(2)}) async-start(), calls=%async_computation.2 | async-start | bytes 262144 | tf_op jit(solution)/shard_map/psum | solution.py:51
  628.0 4.5 copy-start.16
  632.5 4.5 copy-start.10
  637.0 4.5 copy-start.7
  645.9 159.8 %all-reduce.19.cloned.1.call-start = ((), (), s32[]{:S(2)}) async-start(), calls=%async_computation.1 | async-start | bytes 262144 | tf_op jit(solution)/shard_map/psum | solution.py:51
  717.2 4.5 copy-start.19
  721.7 4.5 copy-start.18
  726.2 4.5 copy-start.14
  730.7 75.1 %copy-start.23 = (f32[128]{0:T(128)S(1)}, f32[128]{0:T(128)}, u32[]{:S(2)}) copy-start(f32[128]{0:T(128)} %param.11) | copy-start | bytes 1540
  730.7 86.1 %copy-start.25 = (s32[96]{0:T(128)S(1)}, s32[96]{0:T(128)}, u32[]{:S(2)}) copy-start(s32[96]{0:T(128)} %param.16) | copy-start | bytes 1156
  730.7 95.3 %copy-start.1 = (f32[192,128]{1,0:T(8,128)S(1)}, f32[192,128]{1,0:T(8,128)}, u32[]{:S(2)}) copy-start(f32[192,128]{1,0:T(8,128)} %param.14) | copy-start | bytes 294916
  730.7 95.2 %copy-start.20 = (f32[128]{0:T(128)S(1)}, f32[128]{0:T(128)}, u32[]{:S(2)}) copy-start(f32[128]{0:T(128)} %param.13) | copy-start | bytes 1540
  730.7 95.2 %copy-start.21 = (f32[128]{0:T(128)S(1)}, f32[128]{0:T(128)}, u32[]{:S(2)}) copy-start(f32[128]{0:T(128)} %param.12) | copy-start | bytes 1540
  833.4 7.4 copy-start.24
Sparse Core Ops, SparseCore 0:
  10.0 83.3 all-gather.1
  111.4 69.4 all-reduce.32
  199.8 70.3 all-reduce.30
  289.0 70.3 all-reduce.28
  378.3 70.3 all-reduce.26
  467.5 70.4 all-reduce.24
  556.8 70.3 all-reduce.22
  646.1 70.3 all-reduce.20
  735.4 70.3 all-reduce.18
where the time goes:
time: 849 us; the launch traced here: 847 us
  waiting for transfers between devices  637 us (75%)
  matrix products  144 us (17%)
  blocking collectives  26.2 us (3%)
  other arithmetic  19 us (2%)
  between operations  15.8 us (2%)
    psum x8, waiting for transfers between devices, rollout(): change = lax.psum(partial_change, 'tp')  559 us
    dot_general x32, matrix products, rollout(): jnp.einsum('mck,mkh->mch', hidden_one, hid_rows, preferred_element_type=j...  118 us
    all_gather x1, waiting for transfers between devices, on_device(): input_layer = lax.all_gather(w_in, 'tp', axis=2, tiled=True)  77.4 us
    dot_general x32, matrix products, rollout(): jnp.einsum('mck,mks->mcs', hidden_two, out_rows, preferred_element_type=j...  24.4 us
  transfers between devices with their start and end apart: 9, of which 9 were waited for; matrix products, arithmetic and copies ran while one was open for 1% of the time, Pallas kernels for 0%

commit v1 on v0

--- a/solution.py
+++ b/solution.py
@@ -26,7 +26,12 @@
     ).astype(jnp.float32)
     slot_actions = jnp.dot(dispatch, actions, precision=lax.Precision.HIGHEST)
     slot_actions = slot_actions.reshape(member_count, capacity, HORIZON, action_width)
-    input_layer = lax.all_gather(w_in, "tp", axis=2, tiled=True)
+    ring = [w_in]
+    for hop in range(7):
+        ring.append(lax.ppermute(ring[-1], "tp", [(dev, (dev + 1) % 8) for dev in range(8)]))
+    input_layer = jnp.roll(
+        jnp.concatenate(ring[::-1], axis=2), (lax.axis_index("tp") + 1) * ring[0].shape[2], axis=2
+    )
 
     def rollout(first, count):
         layer_in = input_layer[first : first + count]

time: 849 us -> 897 us (1.057)
  local copies, waits for them, and re-layouts: 3.87 us -> 28.7 us
  waiting for transfers between devices: 637 us -> 647 us
  other arithmetic: 19 us -> 28.3 us
    ppermute x0 -> x7, waiting for transfers between devices: none -> 86.8 us  [on_device(): lax.ppermute(ring[-1], 'tp', [(dev, (dev + 1) % 8) for dev in range(8)])]
    all_gather x1 -> x0, waiting for transfers between devices: 77.4 us -> none  [on_device(): input_layer = lax.all_gather(w_in, 'tp', axis=2, tiled=True)]
    unnamed x81 -> x172, local copies, waits for them, and re-layouts: 2.76 us -> 23.1 us
    reduce_sum x20, other arithmetic: 2.29 us -> 11.5 us  [reward_of(): jnp.mean(action * action, axis=-1)]
  transfers between devices with their start and end apart: 9 -> 15, of which waited for: 9 -> 15; matrix products, arithmetic and copies ran while one was open for 1% -> 3% of each run, Pallas kernels for 0% -> 0%
where the time goes in v1:
time: 897 us; the launch traced here: 895 us
  waiting for transfers between devices  647 us (72%)
  matrix products  145 us (16%)
  local copies, waits for them, and re-layouts  28.7 us (3%)
  other arithmetic  28.3 us (3%)
  blocking collectives  26.2 us (3%)
  between operations  16.4 us (2%)
    psum x8, waiting for transfers between devices, rollout(): change = lax.psum(partial_change, 'tp')  560 us
    dot_general x32, matrix products, rollout(): jnp.einsum('mck,mkh->mch', hidden_one, hid_rows, preferred_element_type=j...  119 us
    ppermute x7, waiting for transfers between devices, on_device(): lax.ppermute(ring[-1], 'tp', [(dev, (dev + 1) % 8) for dev in range(8)])  86.8 us
    dot_general x32, matrix products, rollout(): jnp.einsum('mck,mks->mcs', hidden_two, out_rows, preferred_element_type=j...  24.4 us
    unnamed x172, local copies, waits for them, and re-layouts  23.1 us
  transfers between devices with their start and end apart: 15, of which 15 were waited for; matrix products, arithmetic and copies ran while one was open for 3% of the time, Pallas kernels for 0%

profile of v1, /device:TPU:0, one launch (start us, length us, event | category | flops | bytes accessed | tf_op | source)
XLA Modules:
  0.0 895.4 jit_solution(8284034405872690123)
XLA Ops:
  7.2 3.0 collective-permute-start
  10.3 16.6 %collective-permute-done = bf16[4,144,512]{2,1,0:T(8,128)(2,1)S(1)} collective-permute-done((bf16[4,144,512]{2,1,0:T(8,128)(2,1)}, bf16[4,144,512]{2,1,0:T(8,128)(2,1)S(1)}, u32[]{:S(2)}, u32[]{:S(2)}) %collective-permute-start) | collective-permute-done | bytes 589856 | tf_op jit(solution)/shard_map/ppermute | solution.py:31
  26.8 17.2 %collective-permute-done.1 = bf16[4,144,512]{2,1,0:T(8,128)(2,1)S(1)} collective-permute-done((bf16[4,144,512]{2,1,0:T(8,128)(2,1)S(1)}, bf16[4,144,512]{2,1,0:T(8,128)(2,1)S(1)}, u32[]{:S(2)}, u32[]{:S(2)}) %collective-permute-start.1) | collective-permute-done | bytes 589856 | tf_op jit(solution)/shard_map/ppermute | solution.py:31
  44.0 16.3 %collective-permute-done.2 = bf16[4,144,512]{2,1,0:T(8,128)(2,1)S(1)} collective-permute-done((bf16[4,144,512]{2,1,0:T(8,128)(2,1)S(1)}, bf16[4,144,512]{2,1,0:T(8,128)(2,1)S(1)}, u32[]{:S(2)}, u32[]{:S(2)}) %collective-permute-start.2) | collective-permute-done | bytes 589856 | tf_op jit(solution)/shard_map/ppermute | solution.py:31
  62.6 13.2 %collective-permute-done.3 = bf16[4,144,512]{2,1,0:T(8,128)(2,1)S(1)} collective-permute-done((bf16[4,144,512]{2,1,0:T(8,128)(2,1)S(1)}, bf16[4,144,512]{2,1,0:T(8,128)(2,1)S(1)}, u32[]{:S(2)}, u32[]{:S(2)}) %collective-permute-start.3) | collective-permute-done | bytes 589856 | tf_op jit(solution)/shard_map/ppermute | solution.py:31
  78.7 11.9 %collective-permute-done.4 = bf16[4,144,512]{2,1,0:T(8,128)(2,1)} collective-permute-done((bf16[4,144,512]{2,1,0:T(8,128)(2,1)S(1)}, bf16[4,144,512]{2,1,0:T(8,128)(2,1)}, u32[]{:S(2)}, u32[]{:S(2)}) %collective-permute-start.4) | collective-permute-done | bytes 589856 | tf_op jit(solution)/shard_map/ppermute | solution.py:31
  91.4 1.3 multiply_reduce_fusion.63
  94.0 10.6 %collective-permute-done.5 = bf16[4,144,512]{2,1,0:T(8,128)(2,1)} collective-permute-done((bf16[4,144,512]{2,1,0:T(8,128)(2,1)}, bf16[4,144,512]{2,1,0:T(8,128)(2,1)}, u32[]{:S(2)}, u32[]{:S(2)}) %collective-permute-start.5) | collective-permute-done | bytes 589856 | tf_op jit(solution)/shard_map/ppermute | solution.py:31
  104.7 1.3 multiply_reduce_fusion.12
  110.5 1.3 multiply_reduce_fusion.27
  113.0 1.3 multiply_reduce_fusion.55
  114.3 1.3 multiply_reduce_fusion.10
  115.6 1.3 multiply_reduce_fusion.25
  117.9 2.0 constant_dynamic-update-slice_fusion.15
  119.9 2.0 constant_dynamic-update-slice_fusion.14
  121.9 2.0 constant_dynamic-update-slice_fusion.13
  128.5 2.0 constant_dynamic-update-slice_fusion.7
  130.5 2.0 constant_dynamic-update-slice_fusion.6
  132.5 2.0 constant_dynamic-update-slice_fusion.5
  139.1 3.7 multiply_convert_fusion.157
  143.6 3.7 multiply_convert_fusion.85
  148.1 3.7 multiply_convert_fusion.109
  152.6 3.7 multiply_convert_fusion.133
  157.6 70.5 %all-reduce.33.cloned.1.call-done = (f32[1,60,128]{2,1,0:T(8,128)}, f32[1,60,128]{2,1,0:T(8,128)}, f32[1,60,128]{2,1,0:T(8,128)}, f32[1,60,128]{2,1,0:T(8,128)}) async-done(((f32[1,60,128]{2,1,0:T(8,128)}, f32[1,60,128]{2,1,0:T(8,128)}, f32[1,60,128]{2,1,0:T(8,128)}, f32[1,60,128]{2,1,0:T(8,128)}), (f32[1,60,128]{2,1,0:T(8,128)}, f32[1,60,128]{2,1,0:T(8,128)}, f32[1,60,128]{2,1,0:T(8,128)}, ...) | async-done | bytes 122896 | tf_op jit(solution)/shard_map/psum | solution.py:56
  228.9 3.7 multiply_convert_fusion.154
  233.4 3.7 multiply_convert_fusion.82
  238.0 3.7 multiply_convert_fusion.106
  242.5 3.7 multiply_convert_fusion.130
  247.7 69.8 %all-reduce.31.cloned.1.call-done = (f32[1,60,128]{2,1,0:T(8,128)}, f32[1,60,128]{2,1,0:T(8,128)}, f32[1,60,128]{2,1,0:T(8,128)}, f32[1,60,128]{2,1,0:T(8,128)}) async-done(((f32[1,60,128]{2,1,0:T(8,128)}, f32[1,60,128]{2,1,0:T(8,128)}, f32[1,60,128]{2,1,0:T(8,128)}, f32[1,60,128]{2,1,0:T(8,128)}), (f32[1,60,128]{2,1,0:T(8,128)}, f32[1,60,128]{2,1,0:T(8,128)}, f32[1,60,128]{2,1,0:T(8,128)}, ...) | async-done | bytes 122896 | tf_op jit(solution)/shard_map/psum | solution.py:56
  318.3 3.7 multiply_convert_fusion.151
  322.8 3.7 multiply_convert_fusion.79
  327.3 3.7 multiply_convert_fusion.103
  331.8 3.7 multiply_convert_fusion.127
  336.9 69.9 %all-reduce.29.cloned.1.call-done = (f32[1,60,128]{2,1,0:T(8,128)}, f32[1,60,128]{2,1,0:T(8,128)}, f32[1,60,128]{2,1,0:T(8,128)}, f32[1,60,128]{2,1,0:T(8,128)}) async-done(((f32[1,60,128]{2,1,0:T(8,128)}, f32[1,60,128]{2,1,0:T(8,128)}, f32[1,60,128]{2,1,0:T(8,128)}, f32[1,60,128]{2,1,0:T(8,128)}), (f32[1,60,128]{2,1,0:T(8,128)}, f32[1,60,128]{2,1,0:T(8,128)}, f32[1,60,128]{2,1,0:T(8,128)}, ...) | async-done | bytes 122896 | tf_op jit(solution)/shard_map/psum | solution.py:56
  407.6 3.7 multiply_convert_fusion.148
  412.1 3.7 multiply_convert_fusion.76
  416.6 3.7 multiply_convert_fusion.100
  421.1 3.7 multiply_convert_fusion.124
  426.2 69.9 %all-reduce.27.cloned.1.call-done = (f32[1,60,128]{2,1,0:T(8,128)}, f32[1,60,128]{2,1,0:T(8,128)}, f32[1,60,128]{2,1,0:T(8,128)}, f32[1,60,128]{2,1,0:T(8,128)}) async-done(((f32[1,60,128]{2,1,0:T(8,128)}, f32[1,60,128]{2,1,0:T(8,128)}, f32[1,60,128]{2,1,0:T(8,128)}, f32[1,60,128]{2,1,0:T(8,128)}), (f32[1,60,128]{2,1,0:T(8,128)}, f32[1,60,128]{2,1,0:T(8,128)}, f32[1,60,128]{2,1,0:T(8,128)}, ...) | async-done | bytes 122896 | tf_op jit(solution)/shard_map/psum | solution.py:56
  496.8 3.7 multiply_convert_fusion.145
  501.3 3.7 multiply_convert_fusion.73
  505.8 3.7 multiply_convert_fusion.97
  510.3 3.7 multiply_convert_fusion.121
  515.7 69.7 %all-reduce.25.cloned.1.call-done = (f32[1,60,128]{2,1,0:T(8,128)}, f32[1,60,128]{2,1,0:T(8,128)}, f32[1,60,128]{2,1,0:T(8,128)}, f32[1,60,128]{2,1,0:T(8,128)}) async-done(((f32[1,60,128]{2,1,0:T(8,128)}, f32[1,60,128]{2,1,0:T(8,128)}, f32[1,60,128]{2,1,0:T(8,128)}, f32[1,60,128]{2,1,0:T(8,128)}), (f32[1,60,128]{2,1,0:T(8,128)}, f32[1,60,128]{2,1,0:T(8,128)}, f32[1,60,128]{2,1,0:T(8,128)}, ...) | async-done | bytes 122896 | tf_op jit(solution)/shard_map/psum | solution.py:56
  586.1 3.7 multiply_convert_fusion.142
  590.6 3.7 multiply_convert_fusion.70
  595.1 3.7 multiply_convert_fusion.94
  599.6 3.7 multiply_convert_fusion.118
  604.7 70.0 %all-reduce.23.cloned.1.call-done = (f32[1,60,128]{2,1,0:T(8,128)}, f32[1,60,128]{2,1,0:T(8,128)}, f32[1,60,128]{2,1,0:T(8,128)}, f32[1,60,128]{2,1,0:T(8,128)}) async-done(((f32[1,60,128]{2,1,0:T(8,128)}, f32[1,60,128]{2,1,0:T(8,128)}, f32[1,60,128]{2,1,0:T(8,128)}, f32[1,60,128]{2,1,0:T(8,128)}), (f32[1,60,128]{2,1,0:T(8,128)}, f32[1,60,128]{2,1,0:T(8,128)}, f32[1,60,128]{2,1,0:T(8,128)}, ...) | async-done | bytes 122896 | tf_op jit(solution)/shard_map/psum | solution.py:56
  675.4 3.7 multiply_convert_fusion.139
  679.9 3.7 multiply_convert_fusion.67
  684.4 3.7 multiply_convert_fusion.91
  688.9 3.7 multiply_convert_fusion.115
  693.8 70.1 %all-reduce.21.cloned.1.call-done = (f32[1,60,128]{2,1,0:T(8,128)}, f32[1,60,128]{2,1,0:T(8,128)}, f32[1,60,128]{2,1,0:T(8,128)}, f32[1,60,128]{2,1,0:T(8,128)}) async-done(((f32[1,60,128]{2,1,0:T(8,128)}, f32[1,60,128]{2,1,0:T(8,128)}, f32[1,60,128]{2,1,0:T(8,128)}, f32[1,60,128]{2,1,0:T(8,128)}), (f32[1,60,128]{2,1,0:T(8,128)}, f32[1,60,128]{2,1,0:T(8,128)}, f32[1,60,128]{2,1,0:T(8,128)}, ...) | async-done | bytes 122896 | tf_op jit(solution)/shard_map/psum | solution.py:56
  764.7 3.7 multiply_convert_fusion.136
  769.2 3.7 multiply_convert_fusion.64
  773.8 3.7 multiply_convert_fusion.88
  778.4 3.7 multiply_convert_fusion.112
  782.9 70.5 %all-reduce.19.cloned.1.call-done = (f32[1,60,128]{2,1,0:T(8,128)}, f32[1,60,128]{2,1,0:T(8,128)}, f32[1,60,128]{2,1,0:T(8,128)}, f32[1,60,128]{2,1,0:T(8,128)}) async-done(((f32[1,60,128]{2,1,0:T(8,128)}, f32[1,60,128]{2,1,0:T(8,128)}, f32[1,60,128]{2,1,0:T(8,128)}, f32[1,60,128]{2,1,0:T(8,128)}), (f32[1,60,128]{2,1,0:T(8,128)}, f32[1,60,128]{2,1,0:T(8,128)}, f32[1,60,128]{2,1,0:T(8,128)}, ...) | async-done | bytes 122896 | tf_op jit(solution)/shard_map/psum | solution.py:56
  854.6 1.2 multiply_reduce_fusion.33
  856.9 6.3 psum.291
  864.5 7.2 psum.292
  873.8 6.6 all-reduce.9
  881.3 6.0 psum.295
  (296 shorter events, 64.2 us)
Async XLA Ops:
  7.2 120.5 %copy-start.1 = (bf16[4,144,512]{2,1,0:T(8,128)(2,1)S(1)}, bf16[4,144,512]{2,1,0:T(8,128)(2,1)}, u32[]{:S(2)}) copy-start(bf16[4,144,512]{2,1,0:T(8,128)(2,1)} %param.17) | copy-start | bytes 1769476
  7.2 220.9 %all-reduce.33.cloned.1.call-start = ((), (), s32[]{:S(2)}) async-start(), calls=%async_computation.7 | async-start | bytes 262144 | tf_op jit(solution)/shard_map/psum | solution.py:56
  7.2 19.6 %collective-permute-start = (bf16[4,144,512]{2,1,0:T(8,128)(2,1)}, bf16[4,144,512]{2,1,0:T(8,128)(2,1)S(1)}, u32[]{:S(2)}, u32[]{:S(2)}) collective-permute-start(bf16[4,144,512]{2,1,0:T(8,128)(2,1)} %param.17), channel_id=1, source_target_pairs={{0,1},{1,2},{2,3},{3,4},{4,5},{5,6},{6,7},{7,0},{8,9},{9,10},{10,1... | collective-permute-start | bytes 1769480 | tf_op jit(solution)/shard_map/ppermute | solution.py:31
  26.8 17.2 %collective-permute-start.1 = (bf16[4,144,512]{2,1,0:T(8,128)(2,1)S(1)}, bf16[4,144,512]{2,1,0:T(8,128)(2,1)S(1)}, u32[]{:S(2)}, u32[]{:S(2)}) collective-permute-start(bf16[4,144,512]{2,1,0:T(8,128)(2,1)S(1)} %collective-permute-done), channel_id=1, source_target_pairs={{0,1},{1,2},{2,3},{3,4},{4,5},{5,6},{6,7},{7,0},{8,9},{9,10},{10,1... | collective-permute-start | bytes 1769480 | tf_op jit(solution)/shard_map/ppermute | solution.py:31
  44.0 16.3 %collective-permute-start.2 = (bf16[4,144,512]{2,1,0:T(8,128)(2,1)S(1)}, bf16[4,144,512]{2,1,0:T(8,128)(2,1)S(1)}, u32[]{:S(2)}, u32[]{:S(2)}) collective-permute-start(bf16[4,144,512]{2,1,0:T(8,128)(2,1)S(1)} %collective-permute-done.1), channel_id=1, source_target_pairs={{0,1},{1,2},{2,3},{3,4},{4,5},{5,6},{6,7},{7,0},{8,9},{9,10},{10,1... | collective-permute-start | bytes 1769480 | tf_op jit(solution)/shard_map/ppermute | solution.py:31
  60.4 15.5 %collective-permute-start.3 = (bf16[4,144,512]{2,1,0:T(8,128)(2,1)S(1)}, bf16[4,144,512]{2,1,0:T(8,128)(2,1)S(1)}, u32[]{:S(2)}, u32[]{:S(2)}) collective-permute-start(bf16[4,144,512]{2,1,0:T(8,128)(2,1)S(1)} %collective-permute-done.2), channel_id=1, source_target_pairs={{0,1},{1,2},{2,3},{3,4},{4,5},{5,6},{6,7},{7,0},{8,9},{9,10},{10,1... | collective-permute-start | bytes 1769480 | tf_op jit(solution)/shard_map/ppermute | solution.py:31
  75.8 14.7 %collective-permute-start.4 = (bf16[4,144,512]{2,1,0:T(8,128)(2,1)S(1)}, bf16[4,144,512]{2,1,0:T(8,128)(2,1)}, u32[]{:S(2)}, u32[]{:S(2)}) collective-permute-start(bf16[4,144,512]{2,1,0:T(8,128)(2,1)S(1)} %collective-permute-done.3), channel_id=1, source_target_pairs={{0,1},{1,2},{2,3},{3,4},{4,5},{5,6},{6,7},{7,0},{8,9},{9,10},{10,1... | collective-permute-start | bytes 1769480 | tf_op jit(solution)/shard_map/ppermute | solution.py:31
  77.3 51.2 %copy-start.47 = (s32[192]{0:T(256)}, s32[192]{0:T(256)S(1)}, u32[]{:S(2)}) copy-start(s32[192]{0:T(256)S(1)} %convert_add_fusion) | copy-start | bytes 2308
  90.6 14.1 %collective-permute-start.5 = (bf16[4,144,512]{2,1,0:T(8,128)(2,1)}, bf16[4,144,512]{2,1,0:T(8,128)(2,1)}, u32[]{:S(2)}, u32[]{:S(2)}) collective-permute-start(bf16[4,144,512]{2,1,0:T(8,128)(2,1)} %collective-permute-done.4), channel_id=1, source_target_pairs={{0,1},{1,2},{2,3},{3,4},{4,5},{5,6},{6,7},{7,0},{8,9},{9,10},{10,1... | collective-permute-start | bytes 1769480 | tf_op jit(solution)/shard_map/ppermute | solution.py:31
  104.7 13.2 %collective-permute-start.6 = (bf16[4,144,512]{2,1,0:T(8,128)(2,1)}, bf16[4,144,512]{2,1,0:T(8,128)(2,1)}, u32[]{:S(2)}, u32[]{:S(2)}) collective-permute-start(bf16[4,144,512]{2,1,0:T(8,128)(2,1)} %collective-permute-done.5), channel_id=1, source_target_pairs={{0,1},{1,2},{2,3},{3,4},{4,5},{5,6},{6,7},{7,0},{8,9},{9,10},{10,1... | collective-permute-start | bytes 1769480 | tf_op jit(solution)/shard_map/ppermute | solution.py:31
  130.5 12.3 %copy-start = (bf16[4,512,128]{2,1,0:T(8,128)(2,1)S(1)}, bf16[4,512,128]{2,1,0:T(8,128)(2,1)}, u32[]{:S(2)}) copy-start(bf16[4,512,128]{2,1,0:T(8,128)(2,1)} %param.19) | copy-start | bytes 1572868
  139.1 9.0 %copy-start.42 = (bf16[1,60,1,16]{3,1,2,0:T(8,128)(2,1)S(1)}, bf16[1,60,1,16]{3,1,2,0:T(8,128)(2,1)}, u32[]{:S(2)}) copy-start(bf16[1,60,1,16]{3,1,2,0:T(8,128)(2,1)} %copy.116) | copy-start | bytes 5764
  139.1 9.0 %copy-start.63 = (bf16[144]{0:T(256)(128)(2,1)S(1)}, bf16[144]{0:T(256)(128)(2,1)}, u32[]{:S(2)}) copy-start(bf16[144]{0:T(256)(128)(2,1)} %pad.71.clone) | copy-start | bytes 868
  143.6 9.0 %copy-start.43 = (bf16[1,60,1,16]{3,1,2,0:T(8,128)(2,1)S(1)}, bf16[1,60,1,16]{3,1,2,0:T(8,128)(2,1)}, u32[]{:S(2)}) copy-start(bf16[1,60,1,16]{3,1,2,0:T(8,128)(2,1)} %copy.115) | copy-start | bytes 5764
  148.1 9.2 %copy-start.34 = (f32[1,60,1,16]{1,0,3,2:T(1,128)S(1)}, f32[1,60,1,16]{1,0,3,2:T(1,128)}, u32[]{:S(2)}) copy-start(f32[1,60,1,16]{1,0,3,2:T(1,128)} %get-tuple-element.154) | copy-start | bytes 11524
  148.1 9.3 %copy-start.25 = (f32[1,60,1,16]{1,0,3,2:T(1,128)S(1)}, f32[1,60,1,16]{1,0,3,2:T(1,128)}, u32[]{:S(2)}) copy-start(f32[1,60,1,16]{1,0,3,2:T(1,128)} %get-tuple-element.140) | copy-start | bytes 11524
  148.1 80.0 %copy-start.46 = (f32[128]{0:T(128)S(1)}, f32[128]{0:T(128)}, u32[]{:S(2)}) copy-start(f32[128]{0:T(128)} %param.10) | copy-start | bytes 1540
  148.1 80.8 %copy-start.35 = (bf16[60,16]{1,0:T(8,128)(2,1)S(1)}, bf16[60,16]{1,0:T(8,128)(2,1)}, u32[]{:S(2)}) copy-start(bf16[60,16]{1,0:T(8,128)(2,1)} %get-tuple-element.163) | copy-start | bytes 5764
  152.6 80.8 %copy-start.36 = (bf16[60,16]{1,0:T(8,128)(2,1)S(1)}, bf16[60,16]{1,0:T(8,128)(2,1)}, u32[]{:S(2)}) copy-start(bf16[60,16]{1,0:T(8,128)(2,1)} %get-tuple-element.205) | copy-start | bytes 5764
  157.1 160.3 %all-reduce.31.cloned.1.call-start = ((), (), s32[]{:S(2)}) async-start(), calls=%async_computation.6 | async-start | bytes 262144 | tf_op jit(solution)/shard_map/psum | solution.py:56
  233.4 9.1 %copy-start.40 = (bf16[60,16]{1,0:T(8,128)(2,1)S(1)}, bf16[60,16]{1,0:T(8,128)(2,1)}, u32[]{:S(2)}) copy-start(bf16[60,16]{1,0:T(8,128)(2,1)} %get-tuple-element.177) | copy-start | bytes 5764
  237.9 9.4 %copy-start.24 = (f32[1,60,1,16]{1,0,3,2:T(1,128)S(1)}, f32[1,60,1,16]{1,0,3,2:T(1,128)}, u32[]{:S(2)}) copy-start(f32[1,60,1,16]{1,0,3,2:T(1,128)} %get-tuple-element.133) | copy-start | bytes 11524
  237.9 9.5 %copy-start.23 = (f32[1,60,1,16]{1,0,3,2:T(1,128)S(1)}, f32[1,60,1,16]{1,0,3,2:T(1,128)}, u32[]{:S(2)}) copy-start(f32[1,60,1,16]{1,0,3,2:T(1,128)} %get-tuple-element.132) | copy-start | bytes 11524
  237.9 9.6 %copy-start.33 = (f32[1,60,1,16]{1,0,3,2:T(1,128)S(1)}, f32[1,60,1,16]{1,0,3,2:T(1,128)}, u32[]{:S(2)}) copy-start(f32[1,60,1,16]{1,0,3,2:T(1,128)} %get-tuple-element.148) | copy-start | bytes 11524
  237.9 79.6 %copy-start.3 = (f32[1,60,128]{2,1,0:T(8,128)S(1)}, f32[1,60,128]{2,1,0:T(8,128)}, u32[]{:S(2)}) copy-start(f32[1,60,128]{2,1,0:T(8,128)} %get-tuple-element.73) | copy-start | bytes 92164
  237.9 79.6 %copy-start.4 = (f32[1,60,128]{2,1,0:T(8,128)S(1)}, f32[1,60,128]{2,1,0:T(8,128)}, u32[]{:S(2)}) copy-start(f32[1,60,128]{2,1,0:T(8,128)} %get-tuple-element.74) | copy-start | bytes 92164
  237.9 79.5 %copy-start.5 = (f32[1,60,128]{2,1,0:T(8,128)S(1)}, f32[1,60,128]{2,1,0:T(8,128)}, u32[]{:S(2)}) copy-start(f32[1,60,128]{2,1,0:T(8,128)} %get-tuple-element.75) | copy-start | bytes 92164
  237.9 79.5 %copy-start.6 = (f32[1,60,128]{2,1,0:T(8,128)S(1)}, f32[1,60,128]{2,1,0:T(8,128)}, u32[]{:S(2)}) copy-start(f32[1,60,128]{2,1,0:T(8,128)} %get-tuple-element.76) | copy-start | bytes 92164
  238.0 80.4 %copy-start.39 = (bf16[60,16]{1,0:T(8,128)(2,1)S(1)}, bf16[60,16]{1,0:T(8,128)(2,1)}, u32[]{:S(2)}) copy-start(bf16[60,16]{1,0:T(8,128)(2,1)} %get-tuple-element.165) | copy-start | bytes 5764
  242.5 80.3 %copy-start.38 = (bf16[60,16]{1,0:T(8,128)(2,1)S(1)}, bf16[60,16]{1,0:T(8,128)(2,1)}, u32[]{:S(2)}) copy-start(bf16[60,16]{1,0:T(8,128)(2,1)} %get-tuple-element.207) | copy-start | bytes 5764
  247.0 159.8 %all-reduce.29.cloned.1.call-start = ((), (), s32[]{:S(2)}) async-start(), calls=%async_computation.5 | async-start | bytes 262144 | tf_op jit(solution)/shard_map/psum | solution.py:56
  327.3 9.2 %copy-start.32 = (f32[1,60,1,16]{1,0,3,2:T(1,128)S(1)}, f32[1,60,1,16]{1,0,3,2:T(1,128)}, u32[]{:S(2)}) copy-start(f32[1,60,1,16]{1,0,3,2:T(1,128)} %get-tuple-element.153) | copy-start | bytes 11524
  327.3 9.3 %copy-start.31 = (f32[1,60,1,16]{1,0,3,2:T(1,128)S(1)}, f32[1,60,1,16]{1,0,3,2:T(1,128)}, u32[]{:S(2)}) copy-start(f32[1,60,1,16]{1,0,3,2:T(1,128)} %get-tuple-element.152) | copy-start | bytes 11524
  327.3 9.3 %copy-start.22 = (f32[1,60,1,16]{1,0,3,2:T(1,128)S(1)}, f32[1,60,1,16]{1,0,3,2:T(1,128)}, u32[]{:S(2)}) copy-start(f32[1,60,1,16]{1,0,3,2:T(1,128)} %get-tuple-element.139) | copy-start | bytes 11524
  327.3 9.4 %copy-start.21 = (f32[1,60,1,16]{1,0,3,2:T(1,128)S(1)}, f32[1,60,1,16]{1,0,3,2:T(1,128)}, u32[]{:S(2)}) copy-start(f32[1,60,1,16]{1,0,3,2:T(1,128)} %get-tuple-element.138) | copy-start | bytes 11524
  336.3 159.8 %all-reduce.27.cloned.1.call-start = ((), (), s32[]{:S(2)}) async-start(), calls=%async_computation.4 | async-start | bytes 262144 | tf_op jit(solution)/shard_map/psum | solution.py:56
  416.6 9.1 %copy-start.30 = (f32[1,60,1,16]{1,0,3,2:T(1,128)S(1)}, f32[1,60,1,16]{1,0,3,2:T(1,128)}, u32[]{:S(2)}) copy-start(f32[1,60,1,16]{1,0,3,2:T(1,128)} %get-tuple-element.147) | copy-start | bytes 11524
  416.6 9.2 %copy-start.29 = (f32[1,60,1,16]{1,0,3,2:T(1,128)S(1)}, f32[1,60,1,16]{1,0,3,2:T(1,128)}, u32[]{:S(2)}) copy-start(f32[1,60,1,16]{1,0,3,2:T(1,128)} %get-tuple-element.146) | copy-start | bytes 11524
  425.5 159.8 %all-reduce.25.cloned.1.call-start = ((), (), s32[]{:S(2)}) async-start(), calls=%async_computation.3 | async-start | bytes 262144 | tf_op jit(solution)/shard_map/psum | solution.py:56
  501.3 9.0 %copy-start.9 = (f32[1,60,128]{2,1,0:T(8,128)S(1)}, f32[1,60,128]{2,1,0:T(8,128)}, u32[]{:S(2)}) copy-start(f32[1,60,128]{2,1,0:T(8,128)} %get-tuple-element.61) | copy-start | bytes 92164
  505.8 9.4 %copy-start.28 = (f32[1,60,1,16]{1,0,3,2:T(1,128)S(1)}, f32[1,60,1,16]{1,0,3,2:T(1,128)}, u32[]{:S(2)}) copy-start(f32[1,60,1,16]{1,0,3,2:T(1,128)} %get-tuple-element.151) | copy-start | bytes 11524
  505.8 9.5 %copy-start.27 = (f32[1,60,1,16]{1,0,3,2:T(1,128)S(1)}, f32[1,60,1,16]{1,0,3,2:T(1,128)}, u32[]{:S(2)}) copy-start(f32[1,60,1,16]{1,0,3,2:T(1,128)} %get-tuple-element.145) | copy-start | bytes 11524
  514.8 159.8 %all-reduce.23.cloned.1.call-start = ((), (), s32[]{:S(2)}) async-start(), calls=%async_computation.2 | async-start | bytes 262144 | tf_op jit(solution)/shard_map/psum | solution.py:56
  595.1 9.3 %copy-start.26 = (f32[1,60,1,16]{1,0,3,2:T(1,128)S(1)}, f32[1,60,1,16]{1,0,3,2:T(1,128)}, u32[]{:S(2)}) copy-start(f32[1,60,1,16]{1,0,3,2:T(1,128)} %get-tuple-element.157) | copy-start | bytes 11524
  604.1 159.8 %all-reduce.21.cloned.1.call-start = ((), (), s32[]{:S(2)}) async-start(), calls=%async_computation.1 | async-start | bytes 262144 | tf_op jit(solution)/shard_map/psum | solution.py:56
  693.4 160.0 %all-reduce.19.cloned.1.call-start = ((), (), s32[]{:S(2)}) async-start(), calls=%async_computation | async-start | bytes 262144 | tf_op jit(solution)/shard_map/psum | solution.py:56
  769.2 9.2 %copy-start.13 = (f32[1,60,128]{2,1,0:T(8,128)S(1)}, f32[1,60,128]{2,1,0:T(8,128)}, u32[]{:S(2)}) copy-start(f32[1,60,128]{2,1,0:T(8,128)} %get-tuple-element.49) | copy-start | bytes 92164
  773.7 79.7 %copy-start.60 = (f32[128]{0:T(128)S(1)}, f32[128]{0:T(128)}, u32[]{:S(2)}) copy-start(f32[128]{0:T(128)} %param.11) | copy-start | bytes 1540
  773.7 82.1 %copy-start.53 = (f32[60]{0:T(128)S(1)}, f32[60]{0:T(128)}, u32[]{:S(2)}) copy-start(f32[60]{0:T(128)} %get-tuple-element.3) | copy-start | bytes 724
  773.7 82.1 %copy-start.54 = (f32[60]{0:T(128)S(1)}, f32[60]{0:T(128)}, u32[]{:S(2)}) copy-start(f32[60]{0:T(128)} %get-tuple-element.162) | copy-start | bytes 724
  773.7 82.1 %copy-start.59 = (f32[60]{0:T(128)S(1)}, f32[60]{0:T(128)}, u32[]{:S(2)}) copy-start(f32[60]{0:T(128)} %get-tuple-element.164) | copy-start | bytes 724
  773.7 82.1 %copy-start.52 = (f32[60]{0:T(128)S(1)}, f32[60]{0:T(128)}, u32[]{:S(2)}) copy-start(f32[60]{0:T(128)} %get-tuple-element.4) | copy-start | bytes 724
  773.7 82.1 %copy-start.58 = (f32[60]{0:T(128)S(1)}, f32[60]{0:T(128)}, u32[]{:S(2)}) copy-start(f32[60]{0:T(128)} %get-tuple-element.176) | copy-start | bytes 724
  773.7 82.2 %copy-start.51 = (f32[60]{0:T(128)S(1)}, f32[60]{0:T(128)}, u32[]{:S(2)}) copy-start(f32[60]{0:T(128)} %get-tuple-element.5) | copy-start | bytes 724
  773.7 82.2 %copy-start.56 = (f32[60]{0:T(128)S(1)}, f32[60]{0:T(128)}, u32[]{:S(2)}) copy-start(f32[60]{0:T(128)} %get-tuple-element.190) | copy-start | bytes 724
  773.7 82.2 %copy-start.57 = (f32[60]{0:T(128)S(1)}, f32[60]{0:T(128)}, u32[]{:S(2)}) copy-start(f32[60]{0:T(128)} %get-tuple-element.192) | copy-start | bytes 724
  773.8 82.2 %copy-start.49 = (f32[60]{0:T(128)S(1)}, f32[60]{0:T(128)}, u32[]{:S(2)}) copy-start(f32[60]{0:T(128)} %get-tuple-element.6) | copy-start | bytes 724
  773.8 82.2 %copy-start.50 = (f32[60]{0:T(128)S(1)}, f32[60]{0:T(128)}, u32[]{:S(2)}) copy-start(f32[60]{0:T(128)} %get-tuple-element.204) | copy-start | bytes 724
  773.8 82.2 %copy-start.55 = (f32[60]{0:T(128)S(1)}, f32[60]{0:T(128)}, u32[]{:S(2)}) copy-start(f32[60]{0:T(128)} %get-tuple-element.206) | copy-start | bytes 724
  773.8 82.3 %copy-start.48 = (s32[192]{0:T(256)S(1)}, s32[192]{0:T(256)}, u32[]{:S(2)}) copy-start(s32[192]{0:T(256)} %copy-done.47) | copy-start | bytes 2308
  773.8 90.6 %copy-start.62 = (s32[96]{0:T(128)S(1)}, s32[96]{0:T(128)}, u32[]{:S(2)}) copy-start(s32[96]{0:T(128)} %param.16) | copy-start | bytes 1156
  773.8 99.8 %copy-start.2 = (f32[192,128]{1,0:T(8,128)S(1)}, f32[192,128]{1,0:T(8,128)}, u32[]{:S(2)}) copy-start(f32[192,128]{1,0:T(8,128)} %param.14) | copy-start | bytes 294916
  773.8 99.8 %copy-start.44 = (f32[128]{0:T(128)S(1)}, f32[128]{0:T(128)}, u32[]{:S(2)}) copy-start(f32[128]{0:T(128)} %param.13) | copy-start | bytes 1540
  773.8 99.8 %copy-start.45 = (f32[128]{0:T(128)S(1)}, f32[128]{0:T(128)}, u32[]{:S(2)}) copy-start(f32[128]{0:T(128)} %param.12) | copy-start | bytes 1540
  (15 other events, 110.7 us)
Sparse Core Ops, SparseCore 0:
  157.2 70.8 all-reduce.32
  247.1 70.3 all-reduce.30
  336.4 70.3 all-reduce.28
  425.7 70.3 all-reduce.26
  514.9 70.3 all-reduce.24
  604.2 70.3 all-reduce.22
  693.5 70.3 all-reduce.20
  783.0 70.3 all-reduce.18
